TPU v7x, 32 devices: a whole 2x2x4 slice. The times are simulated.
32 devices in a mesh: grp: 4 (over x, core), dev: 8 (over z, y).
Axes of the slice: x: 2, y: 2, z: 4, core: 2. Of those that a mesh axis runs over, the one named last changes fastest.
Arguments:
- fields: float32 [24, 64, 128, 128], P(None, ('grp', 'dev')), may hold values from -6 to 6
- mix_matrix: float32 [24, 24], replicated, may hold values from -1.25 to 1.25
- laplace_matrix: float32 [24, 24], replicated, may hold values from -0.21875 to 0.21875
Outputs:
- rhs: float32 [24, 64, 128, 128], P(None, ('grp', 'dev'))
- weyl: float32 [2, 64, 128, 128], P(None, 'grp', 'dev')
All inputs are finite; a program needn't handle non-finite values.
Results may differ from a plain program's by a relative error of at most 0.0003.
Values sent between devices are 32-bit elements; how exact they have to be, the bound alone decides.
No kernel may reach another device: no remote copies, remote signals or barrier semaphores. Data moves between devices by JAX's collectives and lax.ppermute only.
A program may use at most 192 MiB of HBM per device.

v0:
```python
import functools

import jax
import jax.numpy as jnp
from jax import lax
from jax.experimental import pallas as pl
from jax.experimental.pallas import tpu as pltpu
from jax.sharding import PartitionSpec as P


WEYL_FIELDS = 12
FIRST = {-2: 1.0 / 12.0, -1: -8.0 / 12.0, 1: 8.0 / 12.0, 2: -1.0 / 12.0}
SECOND = {-2: -1.0 / 12.0, -1: 16.0 / 12.0, 0: -30.0 / 12.0, 1: 16.0 / 12.0, 2: -1.0 / 12.0}
TABLE = ((0, 1, 2), (1, 3, 4), (2, 4, 5))
SMEM = functools.partial(pl.BlockSpec, memory_space=pltpu.SMEM)


def plus(left, right):
    if left is None:
        return right
    if right is None:
        return left
    return left + right


def minus(left, right):
    if right is None:
        return left
    if left is None:
        return -right
    return left - right


def weights(zpos, row, shape, ny, nx):
    along_x = lax.broadcasted_iota(jnp.int32, shape, 1).astype(jnp.float32) + (0.5 - 0.5 * nx)
    along_y = (lax.broadcasted_iota(jnp.int32, shape, 0) + row).astype(jnp.float32)
    along_y = along_y + (0.5 - 0.5 * ny)
    square = along_x * along_x + along_y * along_y
    cylinder = jnp.sqrt(square)
    radius = jnp.sqrt(square + zpos * zpos)
    over_s = 1.0 / cylinder
    over_r = 1.0 / radius
    cos = along_x * over_s
    sin = along_y * over_s
    zed = zpos * over_r
    theta = (zed * cos, zed * sin, -cylinder * over_r)
    phi = (-sin, cos, None)
    even = {}
    odd = {}
    for i in range(3):
        for j in range(i, 3):
            scale = 0.5 if i == j else 1.0
            value = theta[i] * theta[j]
            if phi[i] is not None and phi[j] is not None:
                value = value - phi[i] * phi[j]
            even[TABLE[i][j]] = scale * value
            value = None
            if phi[j] is not None:
                value = plus(value, theta[i] * phi[j])
            if phi[i] is not None:
                value = plus(value, theta[j] * phi[i])
            odd[TABLE[i][j]] = None if value is None else scale * value
    return even, odd


def project(tensor, weight):
    total = None
    for index in range(6):
        if tensor[index] is not None and weight[index] is not None:
            total = plus(total, tensor[index] * weight[index])
    return total


def scalar_pair(electric, grad, even, odd):
    curl = []
    for first in range(3):
        row = []
        up = (first + 1) % 3
        down = (first + 2) % 3
        for second in range(3):
            left = None if grad[up] is None else grad[up][TABLE[down][second]]
            right = None if grad[down] is None else grad[down][TABLE[up][second]]
            row.append(minus(left, right))
        curl.append(row)
    magnetic = {}
    for i in range(3):
        for j in range(i, 3):
            if i == j:
                magnetic[TABLE[i][j]] = curl[i][i]
            else:
                value = plus(curl[i][j], curl[j][i])
                magnetic[TABLE[i][j]] = None if value is None else 0.5 * value
    real = project(electric, even) - project(magnetic, odd)
    imag = -project(electric, odd) - project(magnetic, even)
    return real, imag


def local_kernel(fields_ref, beta_ref, zbase_ref, lap_ref, acc_ref, weyl_ref, hess_ref, gx_ref, gy_ref):
    count, depth, ny, nx = fields_ref.shape
    step = pl.program_id(0)

    def derive(g, carry):
        for z in range(depth):
            f = fields_ref[g, z]
            parts = []
            for axis, size in ((1, nx), (0, ny)):
                a1 = pltpu.roll(f, 1, axis)
                b1 = pltpu.roll(f, size - 1, axis)
                a2 = pltpu.roll(f, 2, axis)
                b2 = pltpu.roll(f, size - 2, axis)
                d1 = (8.0 / 12.0) * (b1 - a1) + (1.0 / 12.0) * (a2 - b2)
                d2 = (16.0 / 12.0) * (b1 + a1) - (1.0 / 12.0) * (a2 + b2)
                parts.append((d1, d2))
            lap = parts[0][1] + parts[1][1] - 7.5 * f
            adv = beta_ref[2, z] * parts[0][0] + beta_ref[1, z] * parts[1][0]
            dz = None
            for offset in (-2, -1, 1, 2):
                if 0 <= z + offset < depth:
                    other = fields_ref[g, z + offset]
                    lap = lap + SECOND[offset] * other
                    dz = plus(dz, FIRST[offset] * other)
            if dz is not None:
                adv = adv + beta_ref[0, z] * dz
            lap_ref[g, z] = lap
            acc_ref[g, z] = adv

            @pl.when(step == 0)
            def _():
                hess_ref[g, z] = lap

            @pl.when(step == 1)
            def _():
                gx_ref[g, z] = parts[0][0]
                gy_ref[g, z] = parts[1][0]
        return carry

    lax.fori_loop(0, count, derive, 0)

    tile = 16 if ny % 16 == 0 else 8

    @pl.when(step == 1)
    def _():
        for z in range(depth):
            def weyl_tile(t, carry, z=z):
                row = pl.multiple_of(t * tile, tile)
                rows = pl.ds(row, tile)
                even, odd = weights(zbase_ref[0] + float(z), row, (tile, nx), ny, nx)
                curv = [fields_ref[i, z, rows, :] for i in range(6)]
                trace = curv[0] + curv[3] + curv[5]
                electric = {}
                for i in range(3):
                    for j in range(i, 3):
                        index = TABLE[i][j]
                        value = -0.5 * hess_ref[index, z, rows, :] - trace * curv[index]
                        for m in range(3):
                            value = value + curv[TABLE[i][m]] * curv[TABLE[m][j]]
                        electric[index] = value
                along_z = None
                for offset in (-2, -1, 1, 2):
                    if 0 <= z + offset < depth:
                        term = [FIRST[offset] * fields_ref[i, z + offset, rows, :] for i in range(6)]
                        along_z = term if along_z is None else [p + q for p, q in zip(along_z, term)]
                grad = [
                    [gx_ref[i, z, rows, :] for i in range(6)],
                    [gy_ref[i, z, rows, :] for i in range(6)],
                    along_z,
                ]
                real, imag = scalar_pair(electric, grad, even, odd)
                weyl_ref[0, z, rows, :] = real
                weyl_ref[1, z, rows, :] = imag
                return carry

            lax.fori_loop(0, ny // tile, weyl_tile, 0)


def sides(first_ref, second_ref, parity, g, z, depth):
    found = []
    for offset in (-2, -1, 1, 2):
        at = z + offset
        if 0 <= at < depth:
            continue
        if at < 0:
            value = jnp.where(parity, first_ref[g, depth + at], second_ref[g, depth + at])
        else:
            value = jnp.where(parity, second_ref[g, at - depth], first_ref[g, at - depth])
        found.append((offset, value))
    return found


def weighted(found, coefficients):
    total = None
    for offset, value in found:
        total = plus(total, coefficients[offset] * value)
    return total


def halo_kernel(starts, parity_ref, lapm_ref, beta_ref, acc_ref, *refs):
    out_ref = refs[-1]
    count, depth = acc_ref.shape[:2]
    parity = parity_ref[0] == 1
    for z in range(depth):
        second = []
        first = {}
        for k, start in enumerate(starts):
            r1, r2 = refs[2 * k], refs[2 * k + 1]
            for g in range(r1.shape[0]):
                found = sides(r1, r2, parity, g, z, depth)
                if found:
                    second.append((start + g, weighted(found, SECOND)))
                    first[start + g] = beta_ref[0, z] * weighted(found, FIRST)
        for c in range(count):
            total = acc_ref[c, z]
            if c in first:
                total = total + first[c]
            for g, value in second:
                total = total + lapm_ref[c * count + g] * value
            out_ref[c, z] = total


def weyl_kernel(ny, row0, parity_ref, zbase_ref, local_ref, r1, r2, out_ref):
    depth, tile, nx = local_ref.shape[1:]
    parity = parity_ref[0] == 1
    row = row0 + pl.program_id(0) * tile
    for z in range(depth):
        even, odd = weights(zbase_ref[0] + float(z), row, (tile, nx), ny, nx)
        electric = {}
        along_z = []
        for i in range(6):
            electric[i] = -0.5 * weighted(sides(r1, r2, parity, i, z, depth), SECOND)
            along_z.append(weighted(sides(r1, r2, parity, 6 + i, z, depth), FIRST))
        real, imag = scalar_pair(electric, [None, None, along_z], even, odd)
        out_ref[0, z] = local_ref[0, z] + real
        out_ref[1, z] = local_ref[1, z] + imag


def local_part(fields, zbase):
    count, depth, ny, nx = fields.shape
    whole = jax.ShapeDtypeStruct(fields.shape, fields.dtype)
    spec = pl.BlockSpec((6, depth, ny, nx), lambda g: (g, 0, 0, 0))
    return pl.pallas_call(
        local_kernel,
        grid=(count // 6,),
        out_shape=(whole, whole, jax.ShapeDtypeStruct((2, depth, ny, nx), fields.dtype)),
        in_specs=[spec, pl.BlockSpec((3, depth, ny, nx), lambda g: (4, 0, 0, 0)), SMEM()],
        out_specs=[spec, spec, pl.BlockSpec((2, depth, ny, nx), lambda g: (0, 0, 0, 0))],
        scratch_shapes=[pltpu.VMEM((6, depth, ny, nx), fields.dtype)] * 3,
        name="local_part",
    )(fields, fields, zbase)


def halo_part(starts, row0, rows, parity, lapm, fields, acc, pieces):
    count, depth, _, nx = fields.shape
    tile = 16 if row0 % 16 == 0 and rows % 16 == 0 else 8
    at = row0 // tile
    spec = pl.BlockSpec((count, depth, tile, nx), lambda t: (0, 0, at + t, 0))
    in_specs = [SMEM(), SMEM(), pl.BlockSpec((1, depth, tile, nx), lambda t: (12, 0, at + t, 0)), spec]
    for piece in pieces:
        in_specs.append(pl.BlockSpec((piece.shape[0], depth, tile, nx), lambda t: (0, 0, t, 0)))
    return pl.pallas_call(
        functools.partial(halo_kernel, starts),
        grid=(rows // tile,),
        out_shape=jax.ShapeDtypeStruct(fields.shape, fields.dtype),
        in_specs=in_specs,
        out_specs=spec,
        input_output_aliases={3: 0},
        name="halo_part",
    )(parity, lapm, fields, acc, *pieces)


def weyl_part(row0, rows, parity, zbase, local, pieces):
    _, depth, ny, nx = local.shape
    tile = 16 if row0 % 16 == 0 and rows % 16 == 0 else 8
    at = row0 // tile
    spec = pl.BlockSpec((2, depth, tile, nx), lambda t: (0, 0, at + t, 0))
    in_specs = [SMEM(), SMEM(), spec]
    for piece in pieces:
        in_specs.append(pl.BlockSpec((piece.shape[0], depth, tile, nx), lambda t: (0, 0, t, 0)))
    return pl.pallas_call(
        functools.partial(weyl_kernel, ny, row0),
        grid=(rows // tile,),
        out_shape=jax.ShapeDtypeStruct(local.shape, local.dtype),
        in_specs=in_specs,
        out_specs=spec,
        input_output_aliases={2: 0},
        name="weyl_part",
    )(parity, zbase, local, *pieces)


def row_ranges(ny):
    unit = ny // 8
    return [(0, 2 * unit), (2 * unit, 3 * unit), (5 * unit, 3 * unit)]


def per_device(fields, mix_matrix, laplace_matrix):
    count, depth, ny, nx = fields.shape
    groups = lax.axis_size("grp")
    members = lax.axis_size("dev")
    ring = groups * members
    axes = ("grp", "dev")
    slab = lax.axis_index("grp") * members + lax.axis_index("dev")
    swap = [(i, i + 1 - 2 * (i % 2)) for i in range(ring)]
    onward = [(i, (i + 2 - 4 * (i % 2)) % ring) for i in range(ring)]
    ranges = row_ranges(ny)
    order = [(0, WEYL_FIELDS, j) for j in range(len(ranges))]
    order += [(WEYL_FIELDS, count, j) for j in reversed(range(len(ranges)))]
    pieces = {}
    for begin, end, j in order:
        row0, rows = ranges[j]
        mine = lax.slice(fields, (begin, 0, row0, 0), (end, depth, row0 + rows, nx))
        beside = lax.ppermute(mine, axes, swap)
        pieces[begin, j] = [beside, lax.ppermute(beside, axes, onward)]
    parity = (slab % 2).astype(jnp.int32).reshape(1)
    zbase = ((slab * depth).astype(jnp.float32) + (0.5 - 0.5 * depth * ring)).reshape(1)
    lapm = laplace_matrix.reshape(-1)
    lap, acc, weyl = local_part(fields, zbase)
    acc = acc + (
        jnp.einsum("fg,gzyx->fzyx", mix_matrix, fields, precision=lax.Precision.HIGH)
        + jnp.einsum("fg,gzyx->fzyx", laplace_matrix, lap, precision=lax.Precision.HIGH)
    )
    for j, (row0, rows) in enumerate(ranges):
        weyl = weyl_part(row0, rows, parity, zbase, weyl, pieces[0, j])
    weyl = lax.all_to_all(weyl, "dev", split_axis=2, concat_axis=1, tiled=True)
    for j in reversed(range(len(ranges))):
        row0, rows = ranges[j]
        flat = pieces[0, j] + pieces[WEYL_FIELDS, j]
        acc = halo_part([0, WEYL_FIELDS], row0, rows, parity, lapm, fields, acc, flat)
    return (acc, weyl)


def solution(mesh):
    return jax.shard_map(
        per_device,
        mesh=mesh,
        in_specs=(P(None, ("grp", "dev"), None, None), P(), P()),
        out_specs=(P(None, ("grp", "dev"), None, None), P(None, "grp", "dev", None)),
        check_vma=False,
    )
```

profile of v0, /device:TPU:0, one launch (start us, length us, event | category | flops | bytes accessed | tf_op | source)
XLA Modules:
  0.0 128.1 jit_solution(11403003240096885938)
XLA Ops:
  0.6 0.0 copy-start
  0.6 0.0 copy-start.1
  0.7 1.3 %fusion.7 = (f32[12,2,32,128]{3,2,1,0:T(8,128)S(1)}, f32[12,2,32,128]{3,2,1,0:T(8,128)S(1)}) fusion(f32[24,2,128,128]{3,2,1,0:T(8,128)} %beta_ref.7), kind=kLoop, calls=%fused_computation.8 | loop fusion | bytes 1572864 | tf_op jit(solution)/shard_map/slice | solution.py:309
  2.0 3.1 %collective-permute-start.8 = (f32[12,2,32,128]{3,2,1,0:T(8,128)S(1)}, f32[12,2,32,128]{3,2,1,0:T(8,128)S(1)}, u32[]{:S(2)}, u32[]{:S(2)}) collective-permute-start(f32[12,2,32,128]{3,2,1,0:T(8,128)S(1)} %get-tuple-element.9), channel_id=1, source_target_pairs={{0,1},{1,0},{2,3},{3,2},{4,5},{5,4},{6,7},{7,6},{8,9},{9,8},{10,11... | collective-permute-start | bytes 1179656 | tf_op jit(solution)/shard_map/ppermute | solution.py:310
  5.1 1.8 %fusion.8 = (f32[12,2,48,128]{3,2,1,0:T(8,128)S(1)}, f32[12,2,48,128]{3,2,1,0:T(8,128)S(1)}, f32[12,2,48,128]{3,2,1,0:T(8,128)S(1)}, f32[12,2,48,128]{3,2,1,0:T(8,128)S(1)}) fusion(f32[24,2,128,128]{3,2,1,0:T(8,128)} %beta_ref.7), kind=kLoop, calls=%fused_computation.9 | loop fusion | bytes 4718592 | tf_op jit(solution)/shard_map/slice | solution.py:309
  6.8 0.1 collective-permute-start
  6.9 2.0 %collective-permute-start.4 = (f32[12,2,48,128]{3,2,1,0:T(8,128)S(1)}, f32[12,2,48,128]{3,2,1,0:T(8,128)}, u32[]{:S(2)}, u32[]{:S(2)}) collective-permute-start(f32[12,2,48,128]{3,2,1,0:T(8,128)S(1)} %get-tuple-element.11), channel_id=1, source_target_pairs={{0,1},{1,0},{2,3},{3,2},{4,5},{5,4},{6,7},{7,6},{8,9},{9,8},{10,11... | collective-permute-start | bytes 1769480 | tf_op jit(solution)/shard_map/ppermute | solution.py:310
  8.9 0.1 collective-permute-start.10
  9.0 1.9 %collective-permute-start.2 = (f32[12,2,48,128]{3,2,1,0:T(8,128)S(1)}, f32[12,2,48,128]{3,2,1,0:T(8,128)}, u32[]{:S(2)}, u32[]{:S(2)}) collective-permute-start(f32[12,2,48,128]{3,2,1,0:T(8,128)S(1)} %get-tuple-element.12), channel_id=1, source_target_pairs={{0,1},{1,0},{2,3},{3,2},{4,5},{5,4},{6,7},{7,6},{8,9},{9,8},{10,11... | collective-permute-start | bytes 1769480 | tf_op jit(solution)/shard_map/ppermute | solution.py:310
  10.9 4.1 %collective-permute-done.8.refs_0_.r1 = f32[12,2,32,128]{3,2,1,0:T(8,128)S(1)} collective-permute-done((f32[12,2,32,128]{3,2,1,0:T(8,128)S(1)}, f32[12,2,32,128]{3,2,1,0:T(8,128)S(1)}, u32[]{:S(2)}, u32[]{:S(2)}) %collective-permute-start.8) | collective-permute-done | bytes 393248 | tf_op jit(solution)/shard_map/ppermute | solution.py:310
  15.0 0.0 copy-start.2
  15.0 2.0 %collective-permute-start.6 = (f32[12,2,48,128]{3,2,1,0:T(8,128)S(1)}, f32[12,2,48,128]{3,2,1,0:T(8,128)}, u32[]{:S(2)}, u32[]{:S(2)}) collective-permute-start(f32[12,2,48,128]{3,2,1,0:T(8,128)S(1)} %get-tuple-element.10), channel_id=1, source_target_pairs={{0,1},{1,0},{2,3},{3,2},{4,5},{5,4},{6,7},{7,6},{8,9},{9,8},{10,11... | collective-permute-start | bytes 1769480 | tf_op jit(solution)/shard_map/ppermute | solution.py:310
  17.0 31.7 %collective-permute-done.10.refs_2_ = f32[12,2,32,128]{3,2,1,0:T(8,128)S(1)} collective-permute-done((f32[12,2,32,128]{3,2,1,0:T(8,128)S(1)}, f32[12,2,32,128]{3,2,1,0:T(8,128)S(1)}, u32[]{:S(2)}, u32[]{:S(2)}) %collective-permute-start.10) | collective-permute-done | bytes 393248 | tf_op jit(solution)/shard_map/ppermute | solution.py:310
  48.7 0.0 copy-start.3
  48.7 2.1 %collective-permute-start.9 = (f32[12,2,32,128]{3,2,1,0:T(8,128)S(1)}, f32[12,2,32,128]{3,2,1,0:T(8,128)}, u32[]{:S(2)}, u32[]{:S(2)}) collective-permute-start(f32[12,2,32,128]{3,2,1,0:T(8,128)S(1)} %collective-permute-done.8.refs_0_.r1), channel_id=1, source_target_pairs={{0,2},{1,31},{2,4},{3,1},{4,6},{5,3},{6,8},{7,5},{8,10},{9,7},{10,... | collective-permute-start | bytes 1179656 | tf_op jit(solution)/shard_map/ppermute | solution.py:311
  50.8 0.0 collective-permute-done.refs_0_.r1
  50.8 1.6 %collective-permute-start.1 = (f32[12,2,48,128]{3,2,1,0:T(8,128)}, f32[12,2,48,128]{3,2,1,0:T(8,128)}, u32[]{:S(2)}, u32[]{:S(2)}) collective-permute-start(f32[12,2,48,128]{3,2,1,0:T(8,128)} %collective-permute-done.refs_0_.r1), channel_id=1, source_target_pairs={{0,2},{1,31},{2,4},{3,1},{4,6},{5,3},{6,8},{7,5},{8,10},{9,7},{10,... | collective-permute-start | bytes 1769480 | tf_op jit(solution)/shard_map/ppermute | solution.py:311
  52.4 0.0 collective-permute-done.4.refs_0_.r1
  52.4 0.0 copy-done.3
  52.4 1.6 %collective-permute-start.5 = (f32[12,2,48,128]{3,2,1,0:T(8,128)}, f32[12,2,48,128]{3,2,1,0:T(8,128)}, u32[]{:S(2)}, u32[]{:S(2)}) collective-permute-start(f32[12,2,48,128]{3,2,1,0:T(8,128)} %collective-permute-done.4.refs_0_.r1), channel_id=1, source_target_pairs={{0,2},{1,31},{2,4},{3,1},{4,6},{5,3},{6,8},{7,5},{8,10},{9,7},{10,... | collective-permute-start | bytes 1769480 | tf_op jit(solution)/shard_map/ppermute | solution.py:311
  54.0 0.0 copy-done
  54.0 0.0 copy-done.1
  54.0 4.6 %fusion.3 = f32[24,2,128,128]{3,0,2,1:T(8,128)} fusion(f32[24,2,128,128]{3,2,1,0:T(8,128)S(1)} %copy-done.1, f32[24,24]{1,0:T(8,128)S(1)} %copy-done), kind=kOutput, calls=%fused_computation.4 | convolution fusion | flops 113246208 | bytes 6293760 | tf_op jit(solution)/shard_map/fg,gzyx->fzyx/dot_general | solution.py:317
  58.6 0.0 copy-done.2
  58.6 11.2 %local_part.1 = (f32[24,2,128,128]{3,2,1,0:T(8,128)}, f32[24,2,128,128]{3,2,1,0:T(8,128)}, f32[2,2,128,128]{3,2,1,0:T(8,128)}) custom-call(f32[24,2,128,128]{3,2,1,0:T(8,128)} %beta_ref.7, f32[24,2,128,128]{3,2,1,0:T(8,128)} %beta_ref.7, f32[1]{0:T(128)} %bitcast.1.zbase_ref), custom_call_target="tpu_custom_call" | custom-call | tf_op jit(solution)/shard_map/local_part/pallas_call | solution.py:240
  69.8 0.0 collective-permute-done.2.refs_2_
  69.8 0.1 collective-permute-start.3
  70.0 3.3 %collective-permute-done.6.refs_2_ = f32[12,2,48,128]{3,2,1,0:T(8,128)} collective-permute-done((f32[12,2,48,128]{3,2,1,0:T(8,128)S(1)}, f32[12,2,48,128]{3,2,1,0:T(8,128)}, u32[]{:S(2)}, u32[]{:S(2)}) %collective-permute-start.6) | collective-permute-done | bytes 589856 | tf_op jit(solution)/shard_map/ppermute | solution.py:310
  73.3 1.8 %collective-permute-start.7 = (f32[12,2,48,128]{3,2,1,0:T(8,128)}, f32[12,2,48,128]{3,2,1,0:T(8,128)}, u32[]{:S(2)}, u32[]{:S(2)}) collective-permute-start(f32[12,2,48,128]{3,2,1,0:T(8,128)} %collective-permute-done.6.refs_2_), channel_id=1, source_target_pairs={{0,2},{1,31},{2,4},{3,1},{4,6},{5,3},{6,8},{7,5},{8,10},{9,7},{10,... | collective-permute-start | bytes 1769480 | tf_op jit(solution)/shard_map/ppermute | solution.py:311
  75.1 4.8 %fusion.1 = f32[2,128,128,24]{2,3,1,0:T(8,128)S(1)} fusion(f32[24,2,128,128]{3,2,1,0:T(8,128)} %get-tuple-element.6, f32[24,24]{1,0:T(8,128)} %param.5), kind=kOutput, calls=%fused_computation.2 | convolution fusion | flops 113246208 | bytes 6293760 | tf_op jit(solution)/shard_map/fg,gzyx->fzyx/dot_general | solution.py:318
  79.9 1.4 %reshape.14.lapm_ref = f32[576]{0:T(1024)} reshape(f32[24,24]{1,0:T(8,128)} %param.5) | data formatting | bytes 4608 | tf_op jit(solution)/shard_map/reshape | solution.py:314
  81.3 0.0 collective-permute-done.9.refs_1_.r2
  81.3 1.6 %collective-permute-start.11 = (f32[12,2,32,128]{3,2,1,0:T(8,128)}, f32[12,2,32,128]{3,2,1,0:T(8,128)}, u32[]{:S(2)}, u32[]{:S(2)}) collective-permute-start(f32[12,2,32,128]{3,2,1,0:T(8,128)} %copy-done.3), channel_id=1, source_target_pairs={{0,2},{1,31},{2,4},{3,1},{4,6},{5,3},{6,8},{7,5},{8,10},{9,7},{10,... | collective-permute-start | bytes 1179656 | tf_op jit(solution)/shard_map/ppermute | solution.py:311
  82.9 2.0 %weyl_part.3.local_ref = f32[2,2,128,128]{3,2,1,0:T(8,128)} custom-call(s32[1]{0:T(128)} %bitcast.parity_ref, f32[1]{0:T(128)} %bitcast.1.zbase_ref, f32[2,2,128,128]{3,2,1,0:T(8,128)} %get-tuple-element.7.local_ref, f32[12,2,32,128]{3,2,1,0:T(8,128)} %copy-done.2, f32[12,2,32,128]{3,2,1,0:T(8,128)} %collective-permute-done.9.refs_1_.r2), custom_call_target="tpu_custom_call", output_to_operand_aliasing={{}: (2, {})} | custom-call | tf_op jit(solution)/shard_map/weyl_part/pallas_call | solution.py:278
  84.9 2.5 %collective-permute-done.5.refs_1_.r2 = f32[12,2,48,128]{3,2,1,0:T(8,128)} collective-permute-done((f32[12,2,48,128]{3,2,1,0:T(8,128)}, f32[12,2,48,128]{3,2,1,0:T(8,128)}, u32[]{:S(2)}, u32[]{:S(2)}) %collective-permute-start.5) | collective-permute-done | bytes 589856 | tf_op jit(solution)/shard_map/ppermute | solution.py:311
  87.3 3.0 %weyl_part.4.local_ref = f32[2,2,128,128]{3,2,1,0:T(8,128)} custom-call(s32[1]{0:T(128)} %bitcast.parity_ref, f32[1]{0:T(128)} %bitcast.1.zbase_ref, f32[2,2,128,128]{3,2,1,0:T(8,128)} %weyl_part.3.local_ref, f32[12,2,48,128]{3,2,1,0:T(8,128)} %collective-permute-done.4.refs_0_.r1, ...), custom_call_target="tpu_custom_call", output_to_operand_aliasing={{}: (2, {})} | custom-call | tf_op jit(solution)/shard_map/weyl_part/pallas_call | solution.py:278
  90.3 0.0 collective-permute-done.1.refs_1_.r2
  90.3 3.0 %weyl_part.5 = f32[2,2,128,128]{3,2,1,0:T(8,128)} custom-call(s32[1]{0:T(128)} %bitcast.parity_ref, f32[1]{0:T(128)} %bitcast.1.zbase_ref, f32[2,2,128,128]{3,2,1,0:T(8,128)} %weyl_part.4.local_ref, f32[12,2,48,128]{3,2,1,0:T(8,128)} %collective-permute-done.refs_0_.r1, ...), custom_call_target="tpu_custom_call", output_to_operand_aliasing={{}: (2, {})} | custom-call | tf_op jit(solution)/shard_map/weyl_part/pallas_call | solution.py:278
  93.3 1.9 %copy.20 = f32[2,2,128,128]{3,1,0,2:T(2,128)} copy(f32[2,2,128,128]{3,2,1,0:T(8,128)} %weyl_part.5) | data formatting | bytes 524288 | tf_op jit(solution)/shard_map/weyl_part/pallas_call | solution.py:278
  95.2 6.3 %all-to-all-start = ((f32[2,2,128,128]{3,1,0,2:T(2,128)}), f32[2,2,128,128]{3,1,0,2:T(2,128)S(1)}, u32[]{:S(2)}, u32[]{:S(2)}) async-start(f32[2,2,128,128]{3,1,0,2:T(2,128)} %copy.20), calls=%async_computation | async-start | bytes 524288 | tf_op jit(solution)/shard_map/all_to_all | solution.py:322
  101.5 5.7 %fusion.acc_ref = f32[24,2,128,128]{3,2,1,0:T(8,128)} fusion(f32[24,2,128,128]{3,2,1,0:T(8,128)} %get-tuple-element.5, f32[24,2,128,128]{3,0,2,1:T(8,128)} %fusion.3, f32[2,128,128,24]{2,3,1,0:T(8,128)S(1)} %fusion.1), kind=kLoop, calls=%fused_computation.1 | loop fusion | flops 1572864 | bytes 12582912 | tf_op jit(solution)/shard_map/add | solution.py:316
  107.2 0.0 collective-permute-done.3.refs_3_
  107.2 5.8 %halo_part.3.acc_ref = f32[24,2,128,128]{3,2,1,0:T(8,128)} custom-call(s32[1]{0:T(128)} %bitcast.parity_ref, f32[576]{0:T(1024)} %reshape.14.lapm_ref, f32[24,2,128,128]{3,2,1,0:T(8,128)} %beta_ref.7, f32[24,2,128,128]{3,2,1,0:T(8,128)} %fusion.acc_ref, f32[12,2,48,128]{3,2,1,0:T(8,128)} %collective-permute-done.refs_0_.r1, ...), custom_call_target="tpu_custom_call", output_to_operand_aliasing={{}: (3, {})} | custom-call | tf_op jit(solution)/shard_map/halo_part/pallas_call | solution.py:259
  113.0 0.0 collective-permute-done.7.refs_3_
  113.0 5.8 %halo_part.4.acc_ref = f32[24,2,128,128]{3,2,1,0:T(8,128)} custom-call(s32[1]{0:T(128)} %bitcast.parity_ref, f32[576]{0:T(1024)} %reshape.14.lapm_ref, f32[24,2,128,128]{3,2,1,0:T(8,128)} %beta_ref.7, f32[24,2,128,128]{3,2,1,0:T(8,128)} %halo_part.3.acc_ref, f32[12,2,48,128]{3,2,1,0:T(8,128)} %collective-permute-done.4.refs_0_.r1, ...), custom_call_target="tpu_custom_call", output_to_operand_aliasing={{}: (3, {})} | custom-call | tf_op jit(solution)/shard_map/halo_part/pallas_call | solution.py:259
  118.7 2.4 %collective-permute-done.11.refs_3_ = f32[12,2,32,128]{3,2,1,0:T(8,128)} collective-permute-done((f32[12,2,32,128]{3,2,1,0:T(8,128)}, f32[12,2,32,128]{3,2,1,0:T(8,128)}, u32[]{:S(2)}, u32[]{:S(2)}) %collective-permute-start.11) | collective-permute-done | bytes 393248 | tf_op jit(solution)/shard_map/ppermute | solution.py:311
  121.1 4.3 %halo_part.5 = f32[24,2,128,128]{3,2,1,0:T(8,128)} custom-call(s32[1]{0:T(128)} %bitcast.parity_ref, f32[576]{0:T(1024)} %reshape.14.lapm_ref, f32[24,2,128,128]{3,2,1,0:T(8,128)} %beta_ref.7, f32[24,2,128,128]{3,2,1,0:T(8,128)} %halo_part.4.acc_ref, f32[12,2,32,128]{3,2,1,0:T(8,128)} %copy-done.2, ...), custom_call_target="tpu_custom_call", output_to_operand_aliasing={{}: (3, {})} | custom-call | tf_op jit(solution)/shard_map/halo_part/pallas_call | solution.py:259
  125.5 1.9 %all-to-all-done = f32[2,2,128,128]{3,1,0,2:T(2,128)S(1)} async-done(((f32[2,2,128,128]{3,1,0,2:T(2,128)}), f32[2,2,128,128]{3,1,0,2:T(2,128)S(1)}, u32[]{:S(2)}, u32[]{:S(2)}) %all-to-all-start) | async-done | bytes 262176 | tf_op jit(solution)/shard_map/all_to_all | solution.py:322
  127.4 0.7 copy.21
Async XLA Ops:
  0.6 53.3 %copy-start = (f32[24,24]{1,0:T(8,128)S(1)}, f32[24,24]{1,0:T(8,128)}, u32[]{:S(2)}) copy-start(f32[24,24]{1,0:T(8,128)} %param.4) | copy-start | bytes 6916
  0.6 53.3 %copy-start.1 = (f32[24,2,128,128]{3,2,1,0:T(8,128)S(1)}, f32[24,2,128,128]{3,2,1,0:T(8,128)}, u32[]{:S(2)}) copy-start(f32[24,2,128,128]{3,2,1,0:T(8,128)} %beta_ref.7) | copy-start | bytes 9437188
  2.0 13.0 %collective-permute-start.8 = (f32[12,2,32,128]{3,2,1,0:T(8,128)S(1)}, f32[12,2,32,128]{3,2,1,0:T(8,128)S(1)}, u32[]{:S(2)}, u32[]{:S(2)}) collective-permute-start(f32[12,2,32,128]{3,2,1,0:T(8,128)S(1)} %get-tuple-element.9), channel_id=1, source_target_pairs={{0,1},{1,0},{2,3},{3,2},{4,5},{5,4},{6,7},{7,6},{8,9},{9,8},{10,11... | collective-permute-start | bytes 1179656 | tf_op jit(solution)/shard_map/ppermute | solution.py:310
  6.8 44.0 %collective-permute-start = (f32[12,2,48,128]{3,2,1,0:T(8,128)S(1)}, f32[12,2,48,128]{3,2,1,0:T(8,128)}, u32[]{:S(2)}, u32[]{:S(2)}) collective-permute-start(f32[12,2,48,128]{3,2,1,0:T(8,128)S(1)} %get-tuple-element.13), channel_id=1, source_target_pairs={{0,1},{1,0},{2,3},{3,2},{4,5},{5,4},{6,7},{7,6},{8,9},{9,8},{10,11... | collective-permute-start | bytes 1769480 | tf_op jit(solution)/shard_map/ppermute | solution.py:310
  6.9 45.5 %collective-permute-start.4 = (f32[12,2,48,128]{3,2,1,0:T(8,128)S(1)}, f32[12,2,48,128]{3,2,1,0:T(8,128)}, u32[]{:S(2)}, u32[]{:S(2)}) collective-permute-start(f32[12,2,48,128]{3,2,1,0:T(8,128)S(1)} %get-tuple-element.11), channel_id=1, source_target_pairs={{0,1},{1,0},{2,3},{3,2},{4,5},{5,4},{6,7},{7,6},{8,9},{9,8},{10,11... | collective-permute-start | bytes 1769480 | tf_op jit(solution)/shard_map/ppermute | solution.py:310
  8.9 39.8 %collective-permute-start.10 = (f32[12,2,32,128]{3,2,1,0:T(8,128)S(1)}, f32[12,2,32,128]{3,2,1,0:T(8,128)S(1)}, u32[]{:S(2)}, u32[]{:S(2)}) collective-permute-start(f32[12,2,32,128]{3,2,1,0:T(8,128)S(1)} %get-tuple-element.8), channel_id=1, source_target_pairs={{0,1},{1,0},{2,3},{3,2},{4,5},{5,4},{6,7},{7,6},{8,9},{9,8},{10,11... | collective-permute-start | bytes 1179656 | tf_op jit(solution)/shard_map/ppermute | solution.py:310
  9.0 60.8 %collective-permute-start.2 = (f32[12,2,48,128]{3,2,1,0:T(8,128)S(1)}, f32[12,2,48,128]{3,2,1,0:T(8,128)}, u32[]{:S(2)}, u32[]{:S(2)}) collective-permute-start(f32[12,2,48,128]{3,2,1,0:T(8,128)S(1)} %get-tuple-element.12), channel_id=1, source_target_pairs={{0,1},{1,0},{2,3},{3,2},{4,5},{5,4},{6,7},{7,6},{8,9},{9,8},{10,11... | collective-permute-start | bytes 1769480 | tf_op jit(solution)/shard_map/ppermute | solution.py:310
  15.0 43.6 %copy-start.2 = (f32[12,2,32,128]{3,2,1,0:T(8,128)}, f32[12,2,32,128]{3,2,1,0:T(8,128)S(1)}, u32[]{:S(2)}) copy-start(f32[12,2,32,128]{3,2,1,0:T(8,128)S(1)} %collective-permute-done.8.refs_0_.r1) | copy-start | bytes 1179652
  15.0 58.2 %collective-permute-start.6 = (f32[12,2,48,128]{3,2,1,0:T(8,128)S(1)}, f32[12,2,48,128]{3,2,1,0:T(8,128)}, u32[]{:S(2)}, u32[]{:S(2)}) collective-permute-start(f32[12,2,48,128]{3,2,1,0:T(8,128)S(1)} %get-tuple-element.10), channel_id=1, source_target_pairs={{0,1},{1,0},{2,3},{3,2},{4,5},{5,4},{6,7},{7,6},{8,9},{9,8},{10,11... | collective-permute-start | bytes 1769480 | tf_op jit(solution)/shard_map/ppermute | solution.py:310
  48.7 3.7 %copy-start.3 = (f32[12,2,32,128]{3,2,1,0:T(8,128)}, f32[12,2,32,128]{3,2,1,0:T(8,128)S(1)}, u32[]{:S(2)}) copy-start(f32[12,2,32,128]{3,2,1,0:T(8,128)S(1)} %collective-permute-done.10.refs_2_) | copy-start | bytes 1179652
  48.7 32.6 %collective-permute-start.9 = (f32[12,2,32,128]{3,2,1,0:T(8,128)S(1)}, f32[12,2,32,128]{3,2,1,0:T(8,128)}, u32[]{:S(2)}, u32[]{:S(2)}) collective-permute-start(f32[12,2,32,128]{3,2,1,0:T(8,128)S(1)} %collective-permute-done.8.refs_0_.r1), channel_id=1, source_target_pairs={{0,2},{1,31},{2,4},{3,1},{4,6},{5,3},{6,8},{7,5},{8,10},{9,7},{10,... | collective-permute-start | bytes 1179656 | tf_op jit(solution)/shard_map/ppermute | solution.py:311
  50.8 39.5 %collective-permute-start.1 = (f32[12,2,48,128]{3,2,1,0:T(8,128)}, f32[12,2,48,128]{3,2,1,0:T(8,128)}, u32[]{:S(2)}, u32[]{:S(2)}) collective-permute-start(f32[12,2,48,128]{3,2,1,0:T(8,128)} %collective-permute-done.refs_0_.r1), channel_id=1, source_target_pairs={{0,2},{1,31},{2,4},{3,1},{4,6},{5,3},{6,8},{7,5},{8,10},{9,7},{10,... | collective-permute-start | bytes 1769480 | tf_op jit(solution)/shard_map/ppermute | solution.py:311
  52.4 34.9 %collective-permute-start.5 = (f32[12,2,48,128]{3,2,1,0:T(8,128)}, f32[12,2,48,128]{3,2,1,0:T(8,128)}, u32[]{:S(2)}, u32[]{:S(2)}) collective-permute-start(f32[12,2,48,128]{3,2,1,0:T(8,128)} %collective-permute-done.4.refs_0_.r1), channel_id=1, source_target_pairs={{0,2},{1,31},{2,4},{3,1},{4,6},{5,3},{6,8},{7,5},{8,10},{9,7},{10,... | collective-permute-start | bytes 1769480 | tf_op jit(solution)/shard_map/ppermute | solution.py:311
  69.8 37.4 %collective-permute-start.3 = (f32[12,2,48,128]{3,2,1,0:T(8,128)}, f32[12,2,48,128]{3,2,1,0:T(8,128)}, u32[]{:S(2)}, u32[]{:S(2)}) collective-permute-start(f32[12,2,48,128]{3,2,1,0:T(8,128)} %collective-permute-done.2.refs_2_), channel_id=1, source_target_pairs={{0,2},{1,31},{2,4},{3,1},{4,6},{5,3},{6,8},{7,5},{8,10},{9,7},{10,... | collective-permute-start | bytes 1769480 | tf_op jit(solution)/shard_map/ppermute | solution.py:311
  73.3 39.7 %collective-permute-start.7 = (f32[12,2,48,128]{3,2,1,0:T(8,128)}, f32[12,2,48,128]{3,2,1,0:T(8,128)}, u32[]{:S(2)}, u32[]{:S(2)}) collective-permute-start(f32[12,2,48,128]{3,2,1,0:T(8,128)} %collective-permute-done.6.refs_2_), channel_id=1, source_target_pairs={{0,2},{1,31},{2,4},{3,1},{4,6},{5,3},{6,8},{7,5},{8,10},{9,7},{10,... | collective-permute-start | bytes 1769480 | tf_op jit(solution)/shard_map/ppermute | solution.py:311
  81.3 39.8 %collective-permute-start.11 = (f32[12,2,32,128]{3,2,1,0:T(8,128)}, f32[12,2,32,128]{3,2,1,0:T(8,128)}, u32[]{:S(2)}, u32[]{:S(2)}) collective-permute-start(f32[12,2,32,128]{3,2,1,0:T(8,128)} %copy-done.3), channel_id=1, source_target_pairs={{0,2},{1,31},{2,4},{3,1},{4,6},{5,3},{6,8},{7,5},{8,10},{9,7},{10,... | collective-permute-start | bytes 1179656 | tf_op jit(solution)/shard_map/ppermute | solution.py:311
  95.2 32.2 %all-to-all-start = ((f32[2,2,128,128]{3,1,0,2:T(2,128)}), f32[2,2,128,128]{3,1,0,2:T(2,128)S(1)}, u32[]{:S(2)}, u32[]{:S(2)}) async-start(f32[2,2,128,128]{3,1,0,2:T(2,128)} %copy.20), calls=%async_computation | async-start | bytes 524288 | tf_op jit(solution)/shard_map/all_to_all | solution.py:322
where the time goes:
time: 129 us; the launch traced here: 128 us
  waiting for transfers between devices  45.9 us (36%)
  Pallas kernels  35 us (27%)
  starting transfers between devices  24.3 us (19%)
  matrix products  9.45 us (7%)
  local copies, waits for them, and re-layouts  7.12 us (6%)
  other arithmetic  5.71 us (4%)
    ppermute x6, waiting for transfers between devices, per_device(): beside = lax.ppermute(mine, axes, swap)  39.1 us
    pallas_call x3, Pallas kernels, halo_part(): pl.pallas_call(functools.partial(halo_kernel, starts), grid=(rows // tile...  15.8 us
    pallas_call x1, Pallas kernels, local_part(): pl.pallas_call(local_kernel, grid=(count // 6,), out_shape=(whole, whole,...  11.2 us
    ppermute x6, starting transfers between devices, per_device(): beside = lax.ppermute(mine, axes, swap)  9.2 us
    ppermute x6, starting transfers between devices, per_device(): pieces[begin, j] = [beside, lax.ppermute(beside, axes, onward)]  8.73 us
    pallas_call x3, Pallas kernels, weyl_part(): pl.pallas_call(functools.partial(weyl_kernel, ny, row0), grid=(rows // ti...  7.94 us
    all_to_all x1, starting transfers between devices, per_device(): weyl = lax.all_to_all(weyl, 'dev', split_axis=2, concat_axis=1, tiled=True)  6.32 us
    add x1, other arithmetic, per_device(): acc + (jnp.einsum('fg,gzyx->fzyx', mix_matrix, fields, precision=lax.Prec...  5.71 us
  transfers between devices with their start and end apart: 13, of which 6 were waited for; matrix products, arithmetic and copies ran while one was open for 16% of the time, Pallas kernels for 27%

commit v1 on v0

--- a/solution.py
+++ b/solution.py
@@ -313,9 +313,9 @@
     zbase = ((slab * depth).astype(jnp.float32) + (0.5 - 0.5 * depth * ring)).reshape(1)
     lapm = laplace_matrix.reshape(-1)
     lap, acc, weyl = local_part(fields, zbase)
-    acc = acc + (
-        jnp.einsum("fg,gzyx->fzyx", mix_matrix, fields, precision=lax.Precision.HIGH)
-        + jnp.einsum("fg,gzyx->fzyx", laplace_matrix, lap, precision=lax.Precision.HIGH)
+    mixed = jnp.einsum("fg,gzyx->fzyx", mix_matrix, fields, precision=lax.Precision.HIGH)
+    acc = (acc + mixed) + jnp.einsum(
+        "fg,gzyx->fzyx", laplace_matrix, lap, precision=lax.Precision.HIGH
     )
     for j, (row0, rows) in enumerate(ranges):
         weyl = weyl_part(row0, rows, parity, zbase, weyl, pieces[0, j])

time: 129 us -> 129 us (level)
  no operation moved by 1% of the time
where the time goes in v1:
time: 129 us; the launch traced here: 128 us
  waiting for transfers between devices  45.8 us (36%)
  Pallas kernels  35 us (27%)
  starting transfers between devices  24.3 us (19%)
  matrix products  9.45 us (7%)
  local copies, waits for them, and re-layouts  7.12 us (6%)
  other arithmetic  5.79 us (4%)
    ppermute x6, waiting for transfers between devices, per_device(): beside = lax.ppermute(mine, axes, swap)  39.1 us
    pallas_call x3, Pallas kernels, halo_part(): pl.pallas_call(functools.partial(halo_kernel, starts), grid=(rows // tile...  15.8 us
    pallas_call x1, Pallas kernels, local_part(): pl.pallas_call(local_kernel, grid=(count // 6,), out_shape=(whole, whole,...  11.2 us
    ppermute x6, starting transfers between devices, per_device(): beside = lax.ppermute(mine, axes, swap)  9.2 us
    ppermute x6, starting transfers between devices, per_device(): pieces[begin, j] = [beside, lax.ppermute(beside, axes, onward)]  8.73 us
    pallas_call x3, Pallas kernels, weyl_part(): pl.pallas_call(functools.partial(weyl_kernel, ny, row0), grid=(rows // ti...  7.94 us
    all_to_all x1, starting transfers between devices, per_device(): weyl = lax.all_to_all(weyl, 'dev', split_axis=2, concat_axis=1, tiled=True)  6.32 us
    add x1, other arithmetic, per_device(): acc + mixed + jnp.einsum('fg,gzyx->fzyx', laplace_matrix, lap, precision=...  5.79 us
  transfers between devices with their start and end apart: 13, of which 6 were waited for; matrix products, arithmetic and copies ran while one was open for 16% of the time, Pallas kernels for 27%

profile of v1, /device:TPU:0, one launch (start us, length us, event | category | flops | bytes accessed | tf_op | source)
XLA Modules:
  0.0 128.1 jit_solution(14786618003412105399)
XLA Ops:
  0.6 0.0 copy-start
  0.6 0.0 copy-start.1
  0.7 1.3 %fusion.6 = (f32[12,2,32,128]{3,2,1,0:T(8,128)S(1)}, f32[12,2,32,128]{3,2,1,0:T(8,128)S(1)}) fusion(f32[24,2,128,128]{3,2,1,0:T(8,128)} %beta_ref.7), kind=kLoop, calls=%fused_computation.8 | loop fusion | bytes 1572864 | tf_op jit(solution)/shard_map/slice | solution.py:309
  2.0 3.1 %collective-permute-start.8 = (f32[12,2,32,128]{3,2,1,0:T(8,128)S(1)}, f32[12,2,32,128]{3,2,1,0:T(8,128)S(1)}, u32[]{:S(2)}, u32[]{:S(2)}) collective-permute-start(f32[12,2,32,128]{3,2,1,0:T(8,128)S(1)} %get-tuple-element.9), channel_id=1, source_target_pairs={{0,1},{1,0},{2,3},{3,2},{4,5},{5,4},{6,7},{7,6},{8,9},{9,8},{10,11... | collective-permute-start | bytes 1179656 | tf_op jit(solution)/shard_map/ppermute | solution.py:310
  5.1 1.8 %fusion.7 = (f32[12,2,48,128]{3,2,1,0:T(8,128)S(1)}, f32[12,2,48,128]{3,2,1,0:T(8,128)S(1)}, f32[12,2,48,128]{3,2,1,0:T(8,128)S(1)}, f32[12,2,48,128]{3,2,1,0:T(8,128)S(1)}) fusion(f32[24,2,128,128]{3,2,1,0:T(8,128)} %beta_ref.7), kind=kLoop, calls=%fused_computation.9 | loop fusion | bytes 4718592 | tf_op jit(solution)/shard_map/slice | solution.py:309
  6.8 0.1 collective-permute-start
  6.9 2.0 %collective-permute-start.4 = (f32[12,2,48,128]{3,2,1,0:T(8,128)S(1)}, f32[12,2,48,128]{3,2,1,0:T(8,128)}, u32[]{:S(2)}, u32[]{:S(2)}) collective-permute-start(f32[12,2,48,128]{3,2,1,0:T(8,128)S(1)} %get-tuple-element.11), channel_id=1, source_target_pairs={{0,1},{1,0},{2,3},{3,2},{4,5},{5,4},{6,7},{7,6},{8,9},{9,8},{10,11... | collective-permute-start | bytes 1769480 | tf_op jit(solution)/shard_map/ppermute | solution.py:310
  8.9 0.1 collective-permute-start.10
  9.0 1.9 %collective-permute-start.2 = (f32[12,2,48,128]{3,2,1,0:T(8,128)S(1)}, f32[12,2,48,128]{3,2,1,0:T(8,128)}, u32[]{:S(2)}, u32[]{:S(2)}) collective-permute-start(f32[12,2,48,128]{3,2,1,0:T(8,128)S(1)} %get-tuple-element.12), channel_id=1, source_target_pairs={{0,1},{1,0},{2,3},{3,2},{4,5},{5,4},{6,7},{7,6},{8,9},{9,8},{10,11... | collective-permute-start | bytes 1769480 | tf_op jit(solution)/shard_map/ppermute | solution.py:310
  10.9 4.1 %collective-permute-done.8.refs_0_.r1 = f32[12,2,32,128]{3,2,1,0:T(8,128)S(1)} collective-permute-done((f32[12,2,32,128]{3,2,1,0:T(8,128)S(1)}, f32[12,2,32,128]{3,2,1,0:T(8,128)S(1)}, u32[]{:S(2)}, u32[]{:S(2)}) %collective-permute-start.8) | collective-permute-done | bytes 393248 | tf_op jit(solution)/shard_map/ppermute | solution.py:310
  15.0 0.0 copy-start.2
  15.0 2.0 %collective-permute-start.6 = (f32[12,2,48,128]{3,2,1,0:T(8,128)S(1)}, f32[12,2,48,128]{3,2,1,0:T(8,128)}, u32[]{:S(2)}, u32[]{:S(2)}) collective-permute-start(f32[12,2,48,128]{3,2,1,0:T(8,128)S(1)} %get-tuple-element.10), channel_id=1, source_target_pairs={{0,1},{1,0},{2,3},{3,2},{4,5},{5,4},{6,7},{7,6},{8,9},{9,8},{10,11... | collective-permute-start | bytes 1769480 | tf_op jit(solution)/shard_map/ppermute | solution.py:310
  17.0 31.7 %collective-permute-done.10.refs_2_ = f32[12,2,32,128]{3,2,1,0:T(8,128)S(1)} collective-permute-done((f32[12,2,32,128]{3,2,1,0:T(8,128)S(1)}, f32[12,2,32,128]{3,2,1,0:T(8,128)S(1)}, u32[]{:S(2)}, u32[]{:S(2)}) %collective-permute-start.10) | collective-permute-done | bytes 393248 | tf_op jit(solution)/shard_map/ppermute | solution.py:310
  48.7 0.0 copy-start.3
  48.7 2.1 %collective-permute-start.9 = (f32[12,2,32,128]{3,2,1,0:T(8,128)S(1)}, f32[12,2,32,128]{3,2,1,0:T(8,128)}, u32[]{:S(2)}, u32[]{:S(2)}) collective-permute-start(f32[12,2,32,128]{3,2,1,0:T(8,128)S(1)} %collective-permute-done.8.refs_0_.r1), channel_id=1, source_target_pairs={{0,2},{1,31},{2,4},{3,1},{4,6},{5,3},{6,8},{7,5},{8,10},{9,7},{10,... | collective-permute-start | bytes 1179656 | tf_op jit(solution)/shard_map/ppermute | solution.py:311
  50.8 0.0 collective-permute-done.refs_0_.r1
  50.8 1.6 %collective-permute-start.1 = (f32[12,2,48,128]{3,2,1,0:T(8,128)}, f32[12,2,48,128]{3,2,1,0:T(8,128)}, u32[]{:S(2)}, u32[]{:S(2)}) collective-permute-start(f32[12,2,48,128]{3,2,1,0:T(8,128)} %collective-permute-done.refs_0_.r1), channel_id=1, source_target_pairs={{0,2},{1,31},{2,4},{3,1},{4,6},{5,3},{6,8},{7,5},{8,10},{9,7},{10,... | collective-permute-start | bytes 1769480 | tf_op jit(solution)/shard_map/ppermute | solution.py:311
  52.4 0.0 collective-permute-done.4.refs_0_.r1
  52.4 0.0 copy-done.3
  52.4 1.6 %collective-permute-start.5 = (f32[12,2,48,128]{3,2,1,0:T(8,128)}, f32[12,2,48,128]{3,2,1,0:T(8,128)}, u32[]{:S(2)}, u32[]{:S(2)}) collective-permute-start(f32[12,2,48,128]{3,2,1,0:T(8,128)} %collective-permute-done.4.refs_0_.r1), channel_id=1, source_target_pairs={{0,2},{1,31},{2,4},{3,1},{4,6},{5,3},{6,8},{7,5},{8,10},{9,7},{10,... | collective-permute-start | bytes 1769480 | tf_op jit(solution)/shard_map/ppermute | solution.py:311
  54.0 0.0 copy-done
  54.0 0.0 copy-done.1
  54.0 4.6 %fusion.2 = f32[24,2,128,128]{3,0,2,1:T(8,128)} fusion(f32[24,2,128,128]{3,2,1,0:T(8,128)S(1)} %copy-done.1, f32[24,24]{1,0:T(8,128)S(1)} %copy-done), kind=kOutput, calls=%fused_computation.4 | convolution fusion | flops 113246208 | bytes 6293760 | tf_op jit(solution)/shard_map/fg,gzyx->fzyx/dot_general | solution.py:316
  58.6 0.0 copy-done.2
  58.6 11.2 %local_part.1 = (f32[24,2,128,128]{3,2,1,0:T(8,128)}, f32[24,2,128,128]{3,2,1,0:T(8,128)}, f32[2,2,128,128]{3,2,1,0:T(8,128)}) custom-call(f32[24,2,128,128]{3,2,1,0:T(8,128)} %beta_ref.7, f32[24,2,128,128]{3,2,1,0:T(8,128)} %beta_ref.7, f32[1]{0:T(128)} %bitcast.1.zbase_ref), custom_call_target="tpu_custom_call" | custom-call | tf_op jit(solution)/shard_map/local_part/pallas_call | solution.py:240
  69.8 0.0 collective-permute-done.2.refs_2_
  69.8 0.1 collective-permute-start.3
  70.0 3.3 %collective-permute-done.6.refs_2_ = f32[12,2,48,128]{3,2,1,0:T(8,128)} collective-permute-done((f32[12,2,48,128]{3,2,1,0:T(8,128)S(1)}, f32[12,2,48,128]{3,2,1,0:T(8,128)}, u32[]{:S(2)}, u32[]{:S(2)}) %collective-permute-start.6) | collective-permute-done | bytes 589856 | tf_op jit(solution)/shard_map/ppermute | solution.py:310
  73.3 1.8 %collective-permute-start.7 = (f32[12,2,48,128]{3,2,1,0:T(8,128)}, f32[12,2,48,128]{3,2,1,0:T(8,128)}, u32[]{:S(2)}, u32[]{:S(2)}) collective-permute-start(f32[12,2,48,128]{3,2,1,0:T(8,128)} %collective-permute-done.6.refs_2_), channel_id=1, source_target_pairs={{0,2},{1,31},{2,4},{3,1},{4,6},{5,3},{6,8},{7,5},{8,10},{9,7},{10,... | collective-permute-start | bytes 1769480 | tf_op jit(solution)/shard_map/ppermute | solution.py:311
  75.1 4.8 %fusion = f32[2,128,128,24]{2,3,1,0:T(8,128)S(1)} fusion(f32[24,2,128,128]{3,2,1,0:T(8,128)} %get-tuple-element.6, f32[24,24]{1,0:T(8,128)} %param.5), kind=kOutput, calls=%fused_computation.1 | convolution fusion | flops 113246208 | bytes 6293760 | tf_op jit(solution)/shard_map/fg,gzyx->fzyx/dot_general | solution.py:317
  79.9 1.4 %reshape.14.lapm_ref = f32[576]{0:T(1024)} reshape(f32[24,24]{1,0:T(8,128)} %param.5) | data formatting | bytes 4608 | tf_op jit(solution)/shard_map/reshape | solution.py:314
  81.3 0.0 collective-permute-done.9.refs_1_.r2
  81.3 1.6 %collective-permute-start.11 = (f32[12,2,32,128]{3,2,1,0:T(8,128)}, f32[12,2,32,128]{3,2,1,0:T(8,128)}, u32[]{:S(2)}, u32[]{:S(2)}) collective-permute-start(f32[12,2,32,128]{3,2,1,0:T(8,128)} %copy-done.3), channel_id=1, source_target_pairs={{0,2},{1,31},{2,4},{3,1},{4,6},{5,3},{6,8},{7,5},{8,10},{9,7},{10,... | collective-permute-start | bytes 1179656 | tf_op jit(solution)/shard_map/ppermute | solution.py:311
  82.9 2.0 %weyl_part.3.local_ref = f32[2,2,128,128]{3,2,1,0:T(8,128)} custom-call(s32[1]{0:T(128)} %bitcast.parity_ref, f32[1]{0:T(128)} %bitcast.1.zbase_ref, f32[2,2,128,128]{3,2,1,0:T(8,128)} %get-tuple-element.7.local_ref, f32[12,2,32,128]{3,2,1,0:T(8,128)} %copy-done.2, f32[12,2,32,128]{3,2,1,0:T(8,128)} %collective-permute-done.9.refs_1_.r2), custom_call_target="tpu_custom_call", output_to_operand_aliasing={{}: (2, {})} | custom-call | tf_op jit(solution)/shard_map/weyl_part/pallas_call | solution.py:278
  84.9 2.5 %collective-permute-done.5.refs_1_.r2 = f32[12,2,48,128]{3,2,1,0:T(8,128)} collective-permute-done((f32[12,2,48,128]{3,2,1,0:T(8,128)}, f32[12,2,48,128]{3,2,1,0:T(8,128)}, u32[]{:S(2)}, u32[]{:S(2)}) %collective-permute-start.5) | collective-permute-done | bytes 589856 | tf_op jit(solution)/shard_map/ppermute | solution.py:311
  87.3 3.0 %weyl_part.4.local_ref = f32[2,2,128,128]{3,2,1,0:T(8,128)} custom-call(s32[1]{0:T(128)} %bitcast.parity_ref, f32[1]{0:T(128)} %bitcast.1.zbase_ref, f32[2,2,128,128]{3,2,1,0:T(8,128)} %weyl_part.3.local_ref, f32[12,2,48,128]{3,2,1,0:T(8,128)} %collective-permute-done.4.refs_0_.r1, ...), custom_call_target="tpu_custom_call", output_to_operand_aliasing={{}: (2, {})} | custom-call | tf_op jit(solution)/shard_map/weyl_part/pallas_call | solution.py:278
  90.3 0.0 collective-permute-done.1.refs_1_.r2
  90.3 3.0 %weyl_part.5 = f32[2,2,128,128]{3,2,1,0:T(8,128)} custom-call(s32[1]{0:T(128)} %bitcast.parity_ref, f32[1]{0:T(128)} %bitcast.1.zbase_ref, f32[2,2,128,128]{3,2,1,0:T(8,128)} %weyl_part.4.local_ref, f32[12,2,48,128]{3,2,1,0:T(8,128)} %collective-permute-done.refs_0_.r1, ...), custom_call_target="tpu_custom_call", output_to_operand_aliasing={{}: (2, {})} | custom-call | tf_op jit(solution)/shard_map/weyl_part/pallas_call | solution.py:278
  93.3 1.9 %copy.20 = f32[2,2,128,128]{3,1,0,2:T(2,128)} copy(f32[2,2,128,128]{3,2,1,0:T(8,128)} %weyl_part.5) | data formatting | bytes 524288 | tf_op jit(solution)/shard_map/weyl_part/pallas_call | solution.py:278
  95.2 6.3 %all-to-all-start = ((f32[2,2,128,128]{3,1,0,2:T(2,128)}), f32[2,2,128,128]{3,1,0,2:T(2,128)S(1)}, u32[]{:S(2)}, u32[]{:S(2)}) async-start(f32[2,2,128,128]{3,1,0,2:T(2,128)} %copy.20), calls=%async_computation | async-start | bytes 524288 | tf_op jit(solution)/shard_map/all_to_all | solution.py:322
  101.5 5.8 %bitcast_add_fusion.acc_ref = f32[24,2,128,128]{3,2,1,0:T(8,128)} fusion(f32[2,128,128,24]{2,3,1,0:T(8,128)S(1)} %fusion, f32[24,2,128,128]{3,2,1,0:T(8,128)} %get-tuple-element.5, f32[24,2,128,128]{3,0,2,1:T(8,128)} %fusion.2), kind=kLoop, calls=%fused_computation | loop fusion | flops 1572864 | bytes 12582912 | tf_op jit(solution)/shard_map/add | solution.py:317
  107.3 0.0 collective-permute-done.3.refs_3_
  107.3 5.8 %halo_part.3.acc_ref = f32[24,2,128,128]{3,2,1,0:T(8,128)} custom-call(s32[1]{0:T(128)} %bitcast.parity_ref, f32[576]{0:T(1024)} %reshape.14.lapm_ref, f32[24,2,128,128]{3,2,1,0:T(8,128)} %beta_ref.7, f32[24,2,128,128]{3,2,1,0:T(8,128)} %bitcast_add_fusion.acc_ref, ...), custom_call_target="tpu_custom_call", output_to_operand_aliasing={{}: (3, {})} | custom-call | tf_op jit(solution)/shard_map/halo_part/pallas_call | solution.py:259
  113.0 0.0 collective-permute-done.7.refs_3_
  113.0 5.8 %halo_part.4.acc_ref = f32[24,2,128,128]{3,2,1,0:T(8,128)} custom-call(s32[1]{0:T(128)} %bitcast.parity_ref, f32[576]{0:T(1024)} %reshape.14.lapm_ref, f32[24,2,128,128]{3,2,1,0:T(8,128)} %beta_ref.7, f32[24,2,128,128]{3,2,1,0:T(8,128)} %halo_part.3.acc_ref, f32[12,2,48,128]{3,2,1,0:T(8,128)} %collective-permute-done.4.refs_0_.r1, ...), custom_call_target="tpu_custom_call", output_to_operand_aliasing={{}: (3, {})} | custom-call | tf_op jit(solution)/shard_map/halo_part/pallas_call | solution.py:259
  118.8 2.3 %collective-permute-done.11.refs_3_ = f32[12,2,32,128]{3,2,1,0:T(8,128)} collective-permute-done((f32[12,2,32,128]{3,2,1,0:T(8,128)}, f32[12,2,32,128]{3,2,1,0:T(8,128)}, u32[]{:S(2)}, u32[]{:S(2)}) %collective-permute-start.11) | collective-permute-done | bytes 393248 | tf_op jit(solution)/shard_map/ppermute | solution.py:311
  121.1 4.3 %halo_part.5 = f32[24,2,128,128]{3,2,1,0:T(8,128)} custom-call(s32[1]{0:T(128)} %bitcast.parity_ref, f32[576]{0:T(1024)} %reshape.14.lapm_ref, f32[24,2,128,128]{3,2,1,0:T(8,128)} %beta_ref.7, f32[24,2,128,128]{3,2,1,0:T(8,128)} %halo_part.4.acc_ref, f32[12,2,32,128]{3,2,1,0:T(8,128)} %copy-done.2, ...), custom_call_target="tpu_custom_call", output_to_operand_aliasing={{}: (3, {})} | custom-call | tf_op jit(solution)/shard_map/halo_part/pallas_call | solution.py:259
  125.5 1.9 %all-to-all-done = f32[2,2,128,128]{3,1,0,2:T(2,128)S(1)} async-done(((f32[2,2,128,128]{3,1,0,2:T(2,128)}), f32[2,2,128,128]{3,1,0,2:T(2,128)S(1)}, u32[]{:S(2)}, u32[]{:S(2)}) %all-to-all-start) | async-done | bytes 262176 | tf_op jit(solution)/shard_map/all_to_all | solution.py:322
  127.4 0.7 copy.21
Async XLA Ops:
  0.6 53.3 %copy-start = (f32[24,24]{1,0:T(8,128)S(1)}, f32[24,24]{1,0:T(8,128)}, u32[]{:S(2)}) copy-start(f32[24,24]{1,0:T(8,128)} %param.4) | copy-start | bytes 6916
  0.6 53.3 %copy-start.1 = (f32[24,2,128,128]{3,2,1,0:T(8,128)S(1)}, f32[24,2,128,128]{3,2,1,0:T(8,128)}, u32[]{:S(2)}) copy-start(f32[24,2,128,128]{3,2,1,0:T(8,128)} %beta_ref.7) | copy-start | bytes 9437188
  2.0 13.0 %collective-permute-start.8 = (f32[12,2,32,128]{3,2,1,0:T(8,128)S(1)}, f32[12,2,32,128]{3,2,1,0:T(8,128)S(1)}, u32[]{:S(2)}, u32[]{:S(2)}) collective-permute-start(f32[12,2,32,128]{3,2,1,0:T(8,128)S(1)} %get-tuple-element.9), channel_id=1, source_target_pairs={{0,1},{1,0},{2,3},{3,2},{4,5},{5,4},{6,7},{7,6},{8,9},{9,8},{10,11... | collective-permute-start | bytes 1179656 | tf_op jit(solution)/shard_map/ppermute | solution.py:310
  6.8 44.0 %collective-permute-start = (f32[12,2,48,128]{3,2,1,0:T(8,128)S(1)}, f32[12,2,48,128]{3,2,1,0:T(8,128)}, u32[]{:S(2)}, u32[]{:S(2)}) collective-permute-start(f32[12,2,48,128]{3,2,1,0:T(8,128)S(1)} %get-tuple-element.13), channel_id=1, source_target_pairs={{0,1},{1,0},{2,3},{3,2},{4,5},{5,4},{6,7},{7,6},{8,9},{9,8},{10,11... | collective-permute-start | bytes 1769480 | tf_op jit(solution)/shard_map/ppermute | solution.py:310
  6.9 45.5 %collective-permute-start.4 = (f32[12,2,48,128]{3,2,1,0:T(8,128)S(1)}, f32[12,2,48,128]{3,2,1,0:T(8,128)}, u32[]{:S(2)}, u32[]{:S(2)}) collective-permute-start(f32[12,2,48,128]{3,2,1,0:T(8,128)S(1)} %get-tuple-element.11), channel_id=1, source_target_pairs={{0,1},{1,0},{2,3},{3,2},{4,5},{5,4},{6,7},{7,6},{8,9},{9,8},{10,11... | collective-permute-start | bytes 1769480 | tf_op jit(solution)/shard_map/ppermute | solution.py:310
  8.9 39.8 %collective-permute-start.10 = (f32[12,2,32,128]{3,2,1,0:T(8,128)S(1)}, f32[12,2,32,128]{3,2,1,0:T(8,128)S(1)}, u32[]{:S(2)}, u32[]{:S(2)}) collective-permute-start(f32[12,2,32,128]{3,2,1,0:T(8,128)S(1)} %get-tuple-element.8), channel_id=1, source_target_pairs={{0,1},{1,0},{2,3},{3,2},{4,5},{5,4},{6,7},{7,6},{8,9},{9,8},{10,11... | collective-permute-start | bytes 1179656 | tf_op jit(solution)/shard_map/ppermute | solution.py:310
  9.0 60.8 %collective-permute-start.2 = (f32[12,2,48,128]{3,2,1,0:T(8,128)S(1)}, f32[12,2,48,128]{3,2,1,0:T(8,128)}, u32[]{:S(2)}, u32[]{:S(2)}) collective-permute-start(f32[12,2,48,128]{3,2,1,0:T(8,128)S(1)} %get-tuple-element.12), channel_id=1, source_target_pairs={{0,1},{1,0},{2,3},{3,2},{4,5},{5,4},{6,7},{7,6},{8,9},{9,8},{10,11... | collective-permute-start | bytes 1769480 | tf_op jit(solution)/shard_map/ppermute | solution.py:310
  15.0 43.6 %copy-start.2 = (f32[12,2,32,128]{3,2,1,0:T(8,128)}, f32[12,2,32,128]{3,2,1,0:T(8,128)S(1)}, u32[]{:S(2)}) copy-start(f32[12,2,32,128]{3,2,1,0:T(8,128)S(1)} %collective-permute-done.8.refs_0_.r1) | copy-start | bytes 1179652
  15.0 58.2 %collective-permute-start.6 = (f32[12,2,48,128]{3,2,1,0:T(8,128)S(1)}, f32[12,2,48,128]{3,2,1,0:T(8,128)}, u32[]{:S(2)}, u32[]{:S(2)}) collective-permute-start(f32[12,2,48,128]{3,2,1,0:T(8,128)S(1)} %get-tuple-element.10), channel_id=1, source_target_pairs={{0,1},{1,0},{2,3},{3,2},{4,5},{5,4},{6,7},{7,6},{8,9},{9,8},{10,11... | collective-permute-start | bytes 1769480 | tf_op jit(solution)/shard_map/ppermute | solution.py:310
  48.7 3.7 %copy-start.3 = (f32[12,2,32,128]{3,2,1,0:T(8,128)}, f32[12,2,32,128]{3,2,1,0:T(8,128)S(1)}, u32[]{:S(2)}) copy-start(f32[12,2,32,128]{3,2,1,0:T(8,128)S(1)} %collective-permute-done.10.refs_2_) | copy-start | bytes 1179652
  48.7 32.6 %collective-permute-start.9 = (f32[12,2,32,128]{3,2,1,0:T(8,128)S(1)}, f32[12,2,32,128]{3,2,1,0:T(8,128)}, u32[]{:S(2)}, u32[]{:S(2)}) collective-permute-start(f32[12,2,32,128]{3,2,1,0:T(8,128)S(1)} %collective-permute-done.8.refs_0_.r1), channel_id=1, source_target_pairs={{0,2},{1,31},{2,4},{3,1},{4,6},{5,3},{6,8},{7,5},{8,10},{9,7},{10,... | collective-permute-start | bytes 1179656 | tf_op jit(solution)/shard_map/ppermute | solution.py:311
  50.8 39.5 %collective-permute-start.1 = (f32[12,2,48,128]{3,2,1,0:T(8,128)}, f32[12,2,48,128]{3,2,1,0:T(8,128)}, u32[]{:S(2)}, u32[]{:S(2)}) collective-permute-start(f32[12,2,48,128]{3,2,1,0:T(8,128)} %collective-permute-done.refs_0_.r1), channel_id=1, source_target_pairs={{0,2},{1,31},{2,4},{3,1},{4,6},{5,3},{6,8},{7,5},{8,10},{9,7},{10,... | collective-permute-start | bytes 1769480 | tf_op jit(solution)/shard_map/ppermute | solution.py:311
  52.4 34.9 %collective-permute-start.5 = (f32[12,2,48,128]{3,2,1,0:T(8,128)}, f32[12,2,48,128]{3,2,1,0:T(8,128)}, u32[]{:S(2)}, u32[]{:S(2)}) collective-permute-start(f32[12,2,48,128]{3,2,1,0:T(8,128)} %collective-permute-done.4.refs_0_.r1), channel_id=1, source_target_pairs={{0,2},{1,31},{2,4},{3,1},{4,6},{5,3},{6,8},{7,5},{8,10},{9,7},{10,... | collective-permute-start | bytes 1769480 | tf_op jit(solution)/shard_map/ppermute | solution.py:311
  69.8 37.5 %collective-permute-start.3 = (f32[12,2,48,128]{3,2,1,0:T(8,128)}, f32[12,2,48,128]{3,2,1,0:T(8,128)}, u32[]{:S(2)}, u32[]{:S(2)}) collective-permute-start(f32[12,2,48,128]{3,2,1,0:T(8,128)} %collective-permute-done.2.refs_2_), channel_id=1, source_target_pairs={{0,2},{1,31},{2,4},{3,1},{4,6},{5,3},{6,8},{7,5},{8,10},{9,7},{10,... | collective-permute-start | bytes 1769480 | tf_op jit(solution)/shard_map/ppermute | solution.py:311
  73.3 39.8 %collective-permute-start.7 = (f32[12,2,48,128]{3,2,1,0:T(8,128)}, f32[12,2,48,128]{3,2,1,0:T(8,128)}, u32[]{:S(2)}, u32[]{:S(2)}) collective-permute-start(f32[12,2,48,128]{3,2,1,0:T(8,128)} %collective-permute-done.6.refs_2_), channel_id=1, source_target_pairs={{0,2},{1,31},{2,4},{3,1},{4,6},{5,3},{6,8},{7,5},{8,10},{9,7},{10,... | collective-permute-start | bytes 1769480 | tf_op jit(solution)/shard_map/ppermute | solution.py:311
  81.3 39.8 %collective-permute-start.11 = (f32[12,2,32,128]{3,2,1,0:T(8,128)}, f32[12,2,32,128]{3,2,1,0:T(8,128)}, u32[]{:S(2)}, u32[]{:S(2)}) collective-permute-start(f32[12,2,32,128]{3,2,1,0:T(8,128)} %copy-done.3), channel_id=1, source_target_pairs={{0,2},{1,31},{2,4},{3,1},{4,6},{5,3},{6,8},{7,5},{8,10},{9,7},{10,... | collective-permute-start | bytes 1179656 | tf_op jit(solution)/shard_map/ppermute | solution.py:311
  95.2 32.2 %all-to-all-start = ((f32[2,2,128,128]{3,1,0,2:T(2,128)}), f32[2,2,128,128]{3,1,0,2:T(2,128)S(1)}, u32[]{:S(2)}, u32[]{:S(2)}) async-start(f32[2,2,128,128]{3,1,0,2:T(2,128)} %copy.20), calls=%async_computation | async-start | bytes 524288 | tf_op jit(solution)/shard_map/all_to_all | solution.py:322
